TPU v7x, 32 devices: a whole 2x2x4 slice. The times are simulated.
32 devices in a mesh: rep: 4 (over x, core), fsdp: 8 (over z, y).
Axes of the slice: x: 2, y: 2, z: 4, core: 2. Of those that a mesh axis runs over, the one named last changes fastest.
Arguments:
- features: bfloat16 [4096, 1280], P(('rep', 'fsdp')), may hold values from -6 to 6
- cotangent: bfloat16 [4096, 1280], P(('rep', 'fsdp')), may hold values from -1 to 1
- clip_lengths: int32 [4, 8], P('rep'), may hold values from 96 to 128, as said below
- group_clips: int32 [4], P('rep'), may hold values from 6 to 8, as said below
- outer_attention: float32 [2, 1280, 5120], P(None, 'fsdp')
- outer_feedforward: float32 [2, 1280, 10240], P(None, 'fsdp')
- outer_vectors: float32 [2, 12, 1280], P(None, None, 'fsdp')
- moments_attention: float32 [4, 2, 1280, 5120], P('rep', None, 'fsdp')
- moments_feedforward: float32 [4, 2, 1280, 10240], P('rep', None, 'fsdp')
- moments_vectors: float32 [4, 2, 12, 1280], P('rep', None, None, 'fsdp')
Outputs:
- block_output: bfloat16 [4096, 1280], P(('rep', 'fsdp'))
- input_grad: float32 [4096, 1280], P(('rep', 'fsdp'))
- group_attention: float32 [4, 3, 1280, 5120], P('rep', None, 'fsdp')
- group_feedforward: float32 [4, 3, 1280, 10240], P('rep', None, 'fsdp')
- group_vectors: float32 [4, 3, 12, 1280], P('rep', None, None, 'fsdp')
- group_weights: float32 [4, 1280, 15372], P('rep', 'fsdp')
- next_attention: float32 [3, 1280, 5120], P(None, 'fsdp')
- next_feedforward: float32 [3, 1280, 10240], P(None, 'fsdp')
- next_vectors: float32 [3, 12, 1280], P(None, None, 'fsdp')
- copy_attention: bfloat16 [1280, 5120], P('fsdp')
- copy_feedforward: bfloat16 [1280, 10240], P('fsdp')
- copy_vectors: bfloat16 [12, 1280], P(None, 'fsdp')
Inputs may be any that keep to these rules, and one draw needn't show every extreme that they name: `clip_lengths`: some clip has exactly 128 valid tokens and some exactly 96. Group g holds clips in its slots 0 to group_clips[g] - 1 and none in the others; some group has all 8 and some 8 - 2.
All inputs are finite; a program needn't handle non-finite values.
Results may differ from a plain program's by a relative error of at most 0.012.
The roundings to bfloat16 on the way count: a program that leaves them out, or rounds other values in their place, can miss the bound.
Values may be sent and summed in bfloat16 or wider, within the bound.
A program may use at most 448 MiB of HBM per device.

v0:
```python
from functools import partial

import jax
import jax.numpy as jnp
from jax import lax
from jax.sharding import PartitionSpec as P

D = 1280
HEADS = 16
HD = 80
FF = 5120
STEP = 3


NORM_EPS = 1e-05
MASKED = -1e30
ADAM_RATE = 0.03
ADAM_DECAY = 0.1
ADAM_BETA = 0.5
ADAM_EPS = 1e-08
OUTER_RATE = 0.7
OUTER_MOMENTUM = 0.5


def contract_last(left, right):
    return lax.dot_general(
        left, right, (((1,), (1,)), ((), ())), preferred_element_type=jnp.float32
    )


def contract_rows(left, right):
    return lax.dot_general(
        left, right, (((0,), (0,)), ((), ())), preferred_element_type=jnp.float32
    )


def normalize(inputs, gain_row, shift_row):
    average = jnp.mean(inputs, axis=-1, keepdims=True)
    centered = inputs - average
    reciprocal = lax.rsqrt(jnp.mean(centered * centered, axis=-1, keepdims=True) + NORM_EPS)
    unit_rows = centered * reciprocal
    return (unit_rows * gain_row + shift_row, unit_rows, reciprocal)


def normalize_back(incoming, unit_rows, reciprocal, gain_row):
    scaled = incoming * gain_row
    centered = scaled - jnp.mean(scaled, axis=-1, keepdims=True)
    return reciprocal * (
        centered - unit_rows * jnp.mean(scaled * unit_rows, axis=-1, keepdims=True)
    )


def adamw_step(weight, gradient, moments, decay_rate):
    first_moment = ADAM_BETA * moments[0] + (1.0 - ADAM_BETA) * gradient
    second_moment = ADAM_BETA * moments[1] + (1.0 - ADAM_BETA) * gradient * gradient
    correction = 1.0 - ADAM_BETA**STEP
    direction = first_moment / correction / (jnp.sqrt(second_moment / correction) + ADAM_EPS)
    return (weight - ADAM_RATE * (direction + decay_rate * weight), first_moment, second_moment)


def outer_step(master, mean_delta, momentum_old):
    momentum = OUTER_MOMENTUM * momentum_old - mean_delta
    outer_next = master - OUTER_RATE * (OUTER_MOMENTUM * momentum - mean_delta)
    return jnp.stack([mean_delta, momentum, outer_next])


def shards(
    features,
    cotangent,
    clip_lengths,
    group_clips,
    outer_attention,
    outer_feedforward,
    outer_vectors,
    moments_attention,
    moments_feedforward,
    moments_vectors,
):
    tokens_here = features.shape[0]
    scale = HD ** (-0.5)
    clip_slot = lax.axis_index("fsdp")
    clip_length = lax.dynamic_index_in_dim(clip_lengths[0], clip_slot, keepdims=False)
    live_clip = clip_slot < group_clips[0]
    positions = jnp.arange(tokens_here, dtype=jnp.int32)
    key_valid = positions < clip_length
    row_valid = key_valid & live_clip
    masters = (outer_attention[0], outer_feedforward[0], outer_vectors[0])
    copies = (
        masters[0].astype(jnp.bfloat16),
        masters[1].astype(jnp.bfloat16),
        masters[2].astype(jnp.bfloat16),
    )
    full_attention, full_feedforward, full_vectors = (
        lax.all_gather(copies[0], "fsdp", axis=0, tiled=True),
        lax.all_gather(copies[1], "fsdp", axis=0, tiled=True),
        lax.all_gather(copies[2], "fsdp", axis=1, tiled=True),
    )
    vectors = full_vectors.astype(jnp.float32)
    inputs = features.astype(jnp.float32)
    normed_one, unit_one, scale_one = normalize(inputs, vectors[0], vectors[1])
    layer_one = normed_one.astype(jnp.bfloat16)
    qkv_bias = jnp.concatenate([vectors[2], jnp.zeros_like(vectors[2]), vectors[3]])
    projected = (
        jnp.dot(layer_one, full_attention[:, : 3 * D], preferred_element_type=jnp.float32)
        + qkv_bias
    ).astype(jnp.bfloat16)
    query_heads = projected[:, :D].reshape(tokens_here, HEADS, HD)
    key_heads = projected[:, D : 2 * D].reshape(tokens_here, HEADS, HD)
    value_heads = projected[:, 2 * D :].reshape(tokens_here, HEADS, HD)

    def score_block():
        raw_scores = (
            jnp.einsum("qhd,khd->hqk", query_heads, key_heads, preferred_element_type=jnp.float32)
            * scale
        )
        return jnp.where(key_valid[None, None, :], raw_scores, MASKED)

    scores = score_block()
    top_score = jnp.max(scores, axis=-1, keepdims=True)
    exponent = jnp.exp(scores - top_score)
    totals = jnp.sum(exponent, axis=-1, keepdims=True)
    attention_probs = exponent / totals
    log_totals = top_score + jnp.log(totals)
    attended = jnp.einsum(
        "hqk,khd->qhd",
        attention_probs.astype(jnp.bfloat16),
        value_heads,
        preferred_element_type=jnp.float32,
    )
    attended = attended.reshape(tokens_here, D).astype(jnp.bfloat16)
    attention_branch = contract_last(attended, full_attention[:, 3 * D :]) + vectors[4]
    middle = inputs + attention_branch
    normed_two, unit_two, scale_two = normalize(middle, vectors[5], vectors[6])
    layer_two = normed_two.astype(jnp.bfloat16)
    pre_activation = jnp.dot(
        layer_two, full_feedforward[:, :FF], preferred_element_type=jnp.float32
    ) + vectors[8:].reshape(FF)
    activation, gelu_backward = jax.vjp(partial(jax.nn.gelu, approximate=False), pre_activation)
    activation_low = activation.astype(jnp.bfloat16)
    feedforward_branch = contract_last(activation_low, full_feedforward[:, FF:]) + vectors[7]
    block_output = (middle + feedforward_branch).astype(jnp.bfloat16)
    back_attention, back_feedforward, back_vectors = (
        lax.all_gather(copies[0], "fsdp", axis=0, tiled=True),
        lax.all_gather(copies[1], "fsdp", axis=0, tiled=True),
        lax.all_gather(copies[2], "fsdp", axis=1, tiled=True),
    )
    gain_rows = back_vectors.astype(jnp.float32)
    upstream = cotangent.astype(jnp.float32) * row_valid[:, None].astype(jnp.float32)
    upstream_low = upstream.astype(jnp.bfloat16)
    grad_down_bias = jnp.sum(upstream_low, axis=0, dtype=jnp.float32)
    grad_activation = jnp.dot(
        upstream_low, back_feedforward[:, FF:], preferred_element_type=jnp.float32
    )
    grad_pre = gelu_backward(grad_activation)[0].astype(jnp.bfloat16)
    grad_up_bias = jnp.sum(grad_pre, axis=0, dtype=jnp.float32)
    grad_two = contract_last(grad_pre, back_feedforward[:, :FF])
    grad_gain_two = jnp.sum(grad_two * unit_two, axis=0)
    grad_shift_two = jnp.sum(grad_two, axis=0)
    grad_middle = upstream + normalize_back(grad_two, unit_two, scale_two, gain_rows[5])
    middle_low = grad_middle.astype(jnp.bfloat16)
    grad_out_bias = jnp.sum(middle_low, axis=0, dtype=jnp.float32)
    grad_attended = jnp.dot(
        middle_low, back_attention[:, 3 * D :], preferred_element_type=jnp.float32
    ).astype(jnp.bfloat16)
    grad_heads = grad_attended.reshape(tokens_here, HEADS, HD)
    attention_probs = jnp.exp(score_block() - log_totals)
    grad_probs = jnp.einsum(
        "qhd,khd->hqk", grad_heads, value_heads, preferred_element_type=jnp.float32
    )
    row_dot = jnp.sum(attention_probs * grad_probs, axis=-1, keepdims=True)
    grad_scores = (attention_probs * (grad_probs - row_dot)).astype(jnp.bfloat16)
    grad_queries = (
        jnp.einsum("hqk,khd->qhd", grad_scores, key_heads, preferred_element_type=jnp.float32)
        * scale
    ).reshape(tokens_here, D)
    grad_keys = (
        jnp.einsum("hqk,qhd->khd", grad_scores, query_heads, preferred_element_type=jnp.float32)
        * scale
    ).reshape(tokens_here, D)
    grad_values = jnp.einsum(
        "hqk,qhd->khd",
        attention_probs.astype(jnp.bfloat16),
        grad_heads,
        preferred_element_type=jnp.float32,
    ).reshape(tokens_here, D)
    grad_qkv = jnp.concatenate([grad_queries, grad_keys, grad_values], axis=1).astype(jnp.bfloat16)
    grad_query_bias = jnp.sum(grad_qkv[:, :D], axis=0, dtype=jnp.float32)
    grad_value_bias = jnp.sum(grad_qkv[:, 2 * D :], axis=0, dtype=jnp.float32)
    grad_one = contract_last(grad_qkv, back_attention[:, : 3 * D])
    grad_gain_one = jnp.sum(grad_one * unit_one, axis=0)
    grad_shift_one = jnp.sum(grad_one, axis=0)
    input_grad = grad_middle + normalize_back(grad_one, unit_one, scale_one, gain_rows[0])
    vector_rows = jnp.stack(
        [
            grad_gain_one,
            grad_shift_one,
            grad_query_bias,
            grad_value_bias,
            grad_out_bias,
            grad_gain_two,
            grad_shift_two,
            grad_down_bias,
        ]
    )
    grad_vectors = jnp.concatenate([vector_rows, grad_up_bias.reshape(4, D)], axis=0)
    owned_attention = lax.psum_scatter(
        jnp.concatenate(
            [contract_rows(layer_one, grad_qkv), contract_rows(middle_low, attended)], axis=1
        ),
        "fsdp",
        scatter_dimension=0,
        tiled=True,
    )
    owned_feedforward = lax.psum_scatter(
        jnp.concatenate(
            [contract_rows(layer_two, grad_pre), contract_rows(upstream_low, activation_low)],
            axis=1,
        ),
        "fsdp",
        scatter_dimension=0,
        tiled=True,
    )
    owned_vectors = lax.psum_scatter(grad_vectors, "fsdp", scatter_dimension=1, tiled=True)
    new_attention, first_attention, second_attention = adamw_step(
        masters[0], owned_attention, moments_attention[0], ADAM_DECAY
    )
    new_feedforward, first_feedforward, second_feedforward = adamw_step(
        masters[1], owned_feedforward, moments_feedforward[0], ADAM_DECAY
    )
    new_vectors, first_vectors, second_vectors = adamw_step(
        masters[2], owned_vectors, moments_vectors[0], 0.0
    )
    summed = (
        lax.psum_scatter(
            (new_attention - masters[0]).astype(jnp.bfloat16),
            "rep",
            scatter_dimension=1,
            tiled=True,
        ).astype(jnp.float32),
        lax.psum_scatter(
            (new_feedforward - masters[1]).astype(jnp.bfloat16),
            "rep",
            scatter_dimension=1,
            tiled=True,
        ).astype(jnp.float32),
        lax.psum_scatter(
            (new_vectors - masters[2]).astype(jnp.bfloat16), "rep", scatter_dimension=0, tiled=True
        ).astype(jnp.float32),
    )
    replicas = lax.axis_size("rep")
    replica_index = lax.axis_index("rep")
    attention_cols = 4 * D // replicas
    feedforward_cols = 2 * FF // replicas
    vector_count = 12 // replicas

    def owned_part(array, dim, count):
        return lax.dynamic_slice_in_dim(array, replica_index * count, count, dim)

    part_attention = outer_step(
        owned_part(masters[0], 1, attention_cols),
        summed[0] / replicas,
        owned_part(outer_attention[1], 1, attention_cols),
    )
    part_feedforward = outer_step(
        owned_part(masters[1], 1, feedforward_cols),
        summed[1] / replicas,
        owned_part(outer_feedforward[1], 1, feedforward_cols),
    )
    part_vectors = outer_step(
        owned_part(masters[2], 0, vector_count),
        summed[2] / replicas,
        owned_part(outer_vectors[1], 0, vector_count),
    )
    next_attention, next_feedforward, next_vectors = (
        lax.all_gather(part_attention, "rep", axis=2, tiled=True),
        lax.all_gather(part_feedforward, "rep", axis=2, tiled=True),
        lax.all_gather(part_vectors, "rep", axis=1, tiled=True),
    )
    copy_attention = next_attention[2].astype(jnp.bfloat16)
    copy_feedforward = next_feedforward[2].astype(jnp.bfloat16)
    copy_vectors = next_vectors[2].astype(jnp.bfloat16)
    group_attention = jnp.stack([owned_attention, first_attention, second_attention])[None]
    group_feedforward = jnp.stack([owned_feedforward, first_feedforward, second_feedforward])[None]
    group_vectors = jnp.stack([owned_vectors, first_vectors, second_vectors])[None]
    group_weights = jnp.concatenate([new_attention, new_feedforward, new_vectors.T], axis=1)[None]
    return (
        block_output,
        input_grad,
        group_attention,
        group_feedforward,
        group_vectors,
        group_weights,
        next_attention,
        next_feedforward,
        next_vectors,
        copy_attention,
        copy_feedforward,
        copy_vectors,
    )


def solution(mesh):
    in_specs = (
        P(("rep", "fsdp"), None),
        P(("rep", "fsdp"), None),
        P("rep", None),
        P("rep"),
        P(None, "fsdp", None),
        P(None, "fsdp", None),
        P(None, None, "fsdp"),
        P("rep", None, "fsdp", None),
        P("rep", None, "fsdp", None),
        P("rep", None, None, "fsdp"),
    )
    out_specs = (
        P(("rep", "fsdp"), None),
        P(("rep", "fsdp"), None),
        P("rep", None, "fsdp", None),
        P("rep", None, "fsdp", None),
        P("rep", None, None, "fsdp"),
        P("rep", "fsdp", None),
        P(None, "fsdp", None),
        P(None, "fsdp", None),
        P(None, None, "fsdp"),
        P("fsdp", None),
        P("fsdp", None),
        P(None, "fsdp"),
    )
    return jax.shard_map(shards, mesh=mesh, in_specs=in_specs, out_specs=out_specs, check_vma=False)
```

profile of v0, /device:TPU:0, one launch (start us, length us, event | category | flops | bytes accessed | tf_op | source)
XLA Modules:
  0.0 2350.7 jit_solution(7769149582330624274)
XLA Ops:
  7.2 3.3 bitcast_convert_fusion.1
  10.6 5.0 bitcast_convert_fusion
  17.1 33.6 %all-gather = bf16[8,160,12]{1,2,0:T(8,128)(2,1)S(1)} all-gather(bf16[1,160,12]{1,2,0:T(8,128)(2,1)S(1)} %copy.142), channel_id=1, replica_groups=mesh['rep'=4,'fsdp'=8] {'fsdp'}, dimensions={0}, use_global_device_ids=true | all-gather | bytes 34560 | tf_op jit(solution)/shard_map/all_gather | solution.py:96
  54.6 141.9 %all-gather.6.cloned.1.call-done = bf16[1280,5120]{1,0:T(8,128)(2,1)} async-done(((bf16[160,5120]{1,0:T(8,128)(2,1)}), bf16[1280,5120]{1,0:T(8,128)(2,1)}) %all-gather.6.cloned.1.call-update) | async-done | bytes 13107216 | tf_op jit(solution)/shard_map/all_gather | solution.py:94
  196.5 5.3 fusion.22
  203.5 3.7 fusion.122
  207.5 489.4 %all-gather.8.cloned.1.call-done = bf16[1280,10240]{1,0:T(8,128)(2,1)} async-done(((bf16[160,10240]{1,0:T(8,128)(2,1)}), bf16[1280,10240]{1,0:T(8,128)(2,1)}) %all-gather.8.cloned.1.call-update) | async-done | bytes 26214416 | tf_op jit(solution)/shard_map/all_gather | solution.py:95
  696.8 5.9 fusion.16
  702.8 11.3 convert_reduce_fusion
  714.1 8.1 multiply_reduce_fusion.1
  722.6 3.3 fusion.57
  725.9 1.9 copy.148
  727.8 1.5 convolution_convert_fusion
  729.3 1.6 multiply_reduce_fusion
  731.9 1.0 fusion.107
  733.0 2.9 fusion.93
  735.9 9.2 pad_maximum_fusion.1
  745.2 13.4 fusion.115
  758.6 12.3 fusion.110
  770.9 35.7 %pad_maximum_fusion = f32[1280,10240]{1,0:T(8,128)} fusion(f32[1280,5120]{1,0:T(8,128)} %fusion.110, f32[1280,5120]{1,0:T(8,128)} %fusion.115), kind=kLoop, calls=%fused_computation | loop fusion | flops 13107200 | bytes 104857600 | tf_op jit(solution)/shard_map/concatenate | solution.py:215
  806.7 356.9 %reduce-scatter.7.cloned.1.call-done = f32[160,5120]{1,0:T(8,128)} async-done(((f32[1280,5120]{1,0:T(8,128)}), f32[160,5120]{1,0:T(8,128)}) %reduce-scatter.7.cloned.1.call-update) | async-done | bytes 3276816 | tf_op jit(solution)/shard_map/reduce_scatter | solution.py:206
  1163.6 9.6 fusion.29
  1173.3 810.7 %reduce-scatter.9.cloned.1.call-done = f32[160,10240]{1,0:T(8,128)} async-done(((f32[1280,10240]{1,0:T(8,128)}), f32[160,10240]{1,0:T(8,128)}) %reduce-scatter.9.cloned.1.call-update) | async-done | bytes 6553616 | tf_op jit(solution)/shard_map/reduce_scatter | solution.py:214
  1984.0 18.2 fusion.15
  2002.5 6.5 fusion.117
  2009.0 6.0 fusion.87
  2015.6 1.1 copy.153
  2016.9 1.7 fusion.90
  2018.6 1.7 pad_maximum_fusion.3
  2020.3 12.6 fusion.116
  2032.9 22.5 reduce-scatter.15.cloned.1.call-done
  2055.5 2.8 fusion.66
  2058.3 2.5 pad_maximum_fusion.2
  2064.5 1.1 fusion.86
  2065.6 13.2 fusion.54
  2078.8 42.8 %reduce-scatter.11.cloned.1.call-done = f32[12,160]{0,1:T(8,128)} async-done(((f32[12,1280]{0,1:T(8,128)}), f32[12,160]{0,1:T(8,128)}) %reduce-scatter.11.cloned.1.call-update) | async-done | bytes 7696 | tf_op jit(solution)/shard_map/reduce_scatter | solution.py:223
  2121.6 1.7 fusion.98
  2126.8 12.0 all-reduce
  2139.2 5.7 all_gather.26
  2145.5 8.3 maximum_bitcast_fusion.2
  2153.9 35.4 %all-gather.10.cloned.1.call-done = f32[3,160,5120]{2,1,0:T(8,128)} async-done(((f32[3,160,1280]{2,1,0:T(8,128)}), f32[3,160,5120]{2,1,0:T(8,128)}) %all-gather.10.cloned.1.call-update) | async-done | bytes 9830416 | tf_op jit(solution)/shard_map/all_gather | solution.py:275
  2189.3 3.3 fusion.61
  2192.6 19.0 maximum_bitcast_fusion
  2212.3 5.5 maximum_bitcast_fusion.1
  2217.8 97.3 %all-gather.12.cloned.1.call-done = f32[3,160,10240]{2,1,0:T(8,128)} async-done(((f32[3,160,2560]{2,1,0:T(8,128)}), f32[3,160,10240]{2,1,0:T(8,128)}) %all-gather.12.cloned.1.call-update) | async-done | bytes 19660816 | tf_op jit(solution)/shard_map/all_gather | solution.py:276
  2315.1 5.0 fusion.26
  2320.1 8.8 copy.180
  2328.9 15.0 copy.181
  (134 shorter events, 17.4 us)
Async XLA Ops:
  7.2 44.4 %copy-start = (s32[1,8]{1,0:T(1,128)S(1)}, s32[1,8]{1,0:T(1,128)}, u32[]{:S(2)}) copy-start(s32[1,8]{1,0:T(1,128)} %param.12) | copy-start | bytes 100
  7.2 189.3 %all-gather.6.cloned.1.call-start = ((), (), s32[]{:S(2)}) async-start(), calls=%async_computation.5 | async-start | bytes 14745600 | tf_op jit(solution)/shard_map/all_gather | solution.py:94
  10.6 686.3 %all-gather.8.cloned.1.call-start = ((), (), s32[]{:S(2)}) async-start(), calls=%async_computation.6 | async-start | bytes 29491200 | tf_op jit(solution)/shard_map/all_gather | solution.py:95
  15.6 0.7 copy-start.17
  15.6 38.6 %copy-start.5 = (bf16[128,1280]{1,0:T(8,128)(2,1)S(1)}, bf16[128,1280]{1,0:T(8,128)(2,1)}, u32[]{:S(2)}) copy-start(bf16[128,1280]{1,0:T(8,128)(2,1)} %param.10) | copy-start | bytes 983044
  15.6 1148.0 %reduce-scatter.7.cloned.1.call-start = ((), (), s32[]{:S(2)}) async-start(), calls=%async_computation.7 | async-start | bytes 29491200 | tf_op jit(solution)/shard_map/reduce_scatter | solution.py:206
  17.1 184.8 %copy-start.9 = (f32[1,12,160]{1,2,0:T(8,128)}, f32[1,12,160]{1,2,0:T(8,128)S(1)}, u32[]{:S(2)}) copy-start(f32[1,12,160]{1,2,0:T(8,128)S(1)} %copy.171) | copy-start | bytes 23044
  202.1 1.3 copy-start.11
  203.5 3.7 copy-start.12
  207.2 538.0 %copy-start.4 = (f32[128,1280]{1,0:T(8,128)}, f32[128,1280]{1,0:T(8,128)S(1)}, u32[]{:S(2)}) copy-start(f32[128,1280]{1,0:T(8,128)S(1)} %get-tuple-element.138) | copy-start | bytes 1966084
  696.8 5.9 copy-start.14
  702.8 11.3 copy-start.21
  714.1 8.1 copy-start.8
  729.2 3.7 copy-start.6
  730.8 1.1 copy-start.13
  745.1 13.5 copy-start.15
  745.2 1238.8 %reduce-scatter.9.cloned.1.call-start = ((), (), s32[]{:S(2)}) async-start(), calls=%async_computation.8 | async-start | bytes 58982400 | tf_op jit(solution)/shard_map/reduce_scatter | solution.py:214
  745.2 13.4 copy-start.22
  806.6 1210.2 %reduce-scatter.13.cloned.1.call-start = ((), (), s32[]{:S(2)}) async-start(), calls=%async_computation.10 | async-start | bytes 2048000 | tf_op jit(solution)/shard_map/reduce_scatter | solution.py:234
  1173.2 882.2 %reduce-scatter.15.cloned.1.call-start = ((), (), s32[]{:S(2)}) async-start(), calls=%async_computation.12 | async-start | bytes 4096000 | tf_op jit(solution)/shard_map/reduce_scatter | solution.py:240
  2002.2 119.3 %reduce-scatter.11.cloned.1.call-start = ((), (), s32[]{:S(2)}) async-start(), calls=%async_computation.9 | async-start | bytes 737280 | tf_op jit(solution)/shard_map/reduce_scatter | solution.py:223
  2002.5 6.5 copy-start.7
  2016.8 172.5 %all-gather.10.cloned.1.call-start = ((), (), s32[]{:S(2)}) async-start(), calls=%async_computation.11 | async-start | bytes 12288000 | tf_op jit(solution)/shard_map/all_gather | solution.py:275
  2020.3 294.8 %all-gather.12.cloned.1.call-start = ((), (), s32[]{:S(2)}) async-start(), calls=%async_computation.13 | async-start | bytes 24576000 | tf_op jit(solution)/shard_map/all_gather | solution.py:276
  2060.8 0.7 copy-start.18
  2060.8 2.4 copy-start.20
  2060.8 4.8 copy-start.19
  2065.6 55.9 %copy-start.10 = (f32[1,12,160]{1,2,0:T(8,128)S(1)}, f32[1,12,160]{1,2,0:T(8,128)}, u32[]{:S(2)}) copy-start(f32[1,12,160]{1,2,0:T(8,128)} %copy-done.9) | copy-start | bytes 23044
  2065.6 79.9 %copy-start.2 = (f32[160,5120]{1,0:T(8,128)S(1)}, f32[160,5120]{1,0:T(8,128)}, u32[]{:S(2)}) copy-start(f32[160,5120]{1,0:T(8,128)} %reduce-scatter.7.cloned.1.call-done) | copy-start | bytes 9830404
  2144.9 9.0 copy-start.16
  2192.6 19.0 slice-start
  2192.6 19.0 slice-start.1
  2192.6 19.7 copy-start.3
  2328.9 15.0 copy-start.1
Sparse Core Ops, SparseCore 0:
  10.8 185.6 all-gather.5
  198.6 498.2 all-gather.7
  745.3 418.2 reduce-scatter.6
  1167.4 816.5 reduce-scatter.8
  1986.9 27.5 reduce-scatter.12
  2016.9 38.5 reduce-scatter.14
  2058.8 62.7 reduce-scatter.10
  2123.1 66.1 all-gather.9
  2190.9 124.1 all-gather.11
where the time goes:
time: 2360 us; the launch traced here: 2350 us
  waiting for transfers between devices  2000 us (85%)
  other arithmetic  120 us (5%)
  matrix products  91.1 us (4%)
  local copies, waits for them, and re-layouts  74.4 us (3%)
  blocking collectives  51.4 us (2%)
    reduce_scatter x1, waiting for transfers between devices, shards(): lax.psum_scatter(jnp.concatenate([contract_rows(layer_two, grad_pre), con...  811 us
    all_gather x1, waiting for transfers between devices, shards(): lax.all_gather(copies[1], 'fsdp', axis=0, tiled=True)  489 us
    reduce_scatter x1, waiting for transfers between devices, shards(): lax.psum_scatter(jnp.concatenate([contract_rows(layer_one, grad_qkv), con...  357 us
    all_gather x1, waiting for transfers between devices, shards(): lax.all_gather(copies[0], 'fsdp', axis=0, tiled=True)  142 us
    all_gather x1, waiting for transfers between devices, shards(): lax.all_gather(part_feedforward, 'rep', axis=2, tiled=True)  97.3 us
  transfers between devices with their start and end apart: 9, of which 8 were waited for; matrix products, arithmetic and copies ran while one was open for 9% of the time, Pallas kernels for 0%

commit v1 on v0

--- a/solution.py
+++ b/solution.py
@@ -3,6 +3,8 @@
 import jax
 import jax.numpy as jnp
 from jax import lax
+from jax.experimental import pallas as pl
+from jax.experimental.pallas import tpu as pltpu
 from jax.sharding import PartitionSpec as P
 
 D = 1280
@@ -64,7 +66,7 @@
     return jnp.stack([mean_delta, momentum, outer_next])
 
 
-def shards(
+def shards_generic(
     features,
     cotangent,
     clip_lengths,
@@ -299,7 +301,775 @@
     )
 
 
+LEN = 128
+TP = 8
+HW = D // TP
+FW = FF // TP
+CW = 4 * HW + 2 * FW
+AUX = 16
+MESH = pl.DeviceIdType.MESH
+BF = jnp.bfloat16
+F32 = jnp.float32
+
+
+def place():
+    r, f = lax.axis_index("rep"), lax.axis_index("fsdp")
+    x, k, c, q = r // 2, r % 2, f // 4, f % 4
+    return r, f, x, k, c, q, 4 * k + q
+
+
+def flip(q, j):
+    low, high = q % 2, q // 2
+    if j & 1:
+        low = 1 - low
+    if j & 2:
+        high = 1 - high
+    return high * 2 + low
+
+
+def remote(src, dst, send, recv, rep, fsdp):
+    return pltpu.make_async_remote_copy(
+        src_ref=src,
+        dst_ref=dst,
+        send_sem=send,
+        recv_sem=recv,
+        device_id={"rep": rep, "fsdp": fsdp},
+        device_id_type=MESH,
+    )
+
+
+def meet(peers):
+    barrier = pltpu.get_barrier_semaphore()
+    for rep, fsdp in peers:
+        pl.semaphore_signal(
+            barrier, inc=1, device_id={"rep": rep, "fsdp": fsdp}, device_id_type=MESH
+        )
+    pl.semaphore_wait(barrier, len(peers))
+
+
+def comm_params(cid):
+    return pltpu.CompilerParams(collective_id=cid, has_side_effects=True)
+
+
+ANY = pl.BlockSpec(memory_space=pl.ANY)
+VM = pl.BlockSpec(memory_space=pltpu.VMEM)
+DMA = pltpu.SemaphoreType.DMA
+
+
+def first_kernel(x_ref, u_ref, w_ref, v_ref, xf, uf, wf, vf, own, sw, rw, ls, sg, rg, sp, rp, sv, rv, so, ro, fo, go):
+    r, f, x, k, c, q, w = place()
+    peers = [(2 * x + (k + kk) % 2, (f + i) % 8) for kk in range(2) for i in range(8) if kk or i]
+    meet(peers + [(2 * (1 - x) + k, f)])
+    pr, pf = 2 * x + c, 4 * k + q
+    swaps = [
+        remote(src, dst.at[f], sw.at[n], rw.at[n], pr, pf)
+        for n, (src, dst) in enumerate(((x_ref, xf), (u_ref, uf)))
+    ]
+    keeps = [
+        pltpu.make_async_copy(src, dst.at[w], ls.at[n])
+        for n, (src, dst) in enumerate(((x_ref, xf), (u_ref, uf)))
+    ]
+
+    @pl.when(k != c)
+    def _():
+        for copy in swaps:
+            copy.start()
+
+    @pl.when(k == c)
+    def _():
+        for copy in keeps:
+            copy.start()
+
+    half = pl.ds(pl.multiple_of(x * (HW // 2), 16), HW // 2)
+    sends = []
+    for i in range(1, 8):
+        to = (f + i) % 8
+        vec = remote(v_ref, vf.at[f], sv.at[i], rv.at[i], r, to)
+        vec.start()
+        out = remote(w_ref.at[to % 4, half], wf.at[f, half], so.at[i], ro.at[i], r, to)
+        out.start()
+        sends += [vec, out]
+    load = pltpu.make_async_copy(w_ref.at[q], own, ls.at[2])
+    load.start()
+    keep_vec = pltpu.make_async_copy(v_ref, vf.at[f], ls.at[3])
+    keep_vec.start()
+    load.wait()
+    keep_own = pltpu.make_async_copy(own, wf.at[f], ls.at[4])
+    keep_own.start()
+
+    partner = 2 * x + 1 - k
+    spread = []
+    for n, dst in enumerate((xf, uf)):
+
+        @pl.when(k != c)
+        def _(n=n):
+            swaps[n].wait_recv()
+
+        @pl.when(k == c)
+        def _(n=n):
+            keeps[n].wait()
+
+        mine = dst.at[w]
+        to_partner = remote(mine, mine, sp.at[n, 0], rp.at[n, 0], partner, f)
+        to_partner.start()
+        near = [
+            remote(mine, mine, sg.at[n, j], rg.at[n, j], r, 4 * c + flip(q, j)) for j in range(1, 4)
+        ]
+        for copy in near:
+            copy.start()
+        spread.append((dst, near, [to_partner]))
+    for n, (dst, near, passed) in enumerate(spread):
+        for j in range(1, 4):
+            near[j - 1].wait_recv()
+            got = dst.at[4 * k + flip(q, j)]
+            copy = remote(got, got, sp.at[n, j], rp.at[n, j], partner, f)
+            copy.start()
+            passed.append(copy)
+    over = []
+    for i in range(1, 8):
+        source = (f + 8 - i) % 8
+        sends[2 * i - 1].wait_recv()
+        got = wf.at[source, half]
+        copy = remote(got, got, fo.at[i], go.at[i], 2 * (1 - x) + k, f)
+        copy.start()
+        over.append(copy)
+    for dst, near, passed in spread:
+        for copy in near:
+            copy.wait_send()
+        for copy in passed:
+            copy.wait()
+    for i in range(1, 8):
+        sends[2 * i - 2].wait()
+        sends[2 * i - 1].wait_send()
+    for copy in over:
+        copy.wait()
+    keep_vec.wait()
+    keep_own.wait()
+
+    @pl.when(k != c)
+    def _():
+        for copy in swaps:
+            copy.wait_send()
+
+
+def first_exchange(xb, ub, wsend, vsend):
+    return pl.pallas_call(
+        first_kernel,
+        name="first_exchange",
+        out_shape=(
+            jax.ShapeDtypeStruct((TP,) + xb.shape, BF),
+            jax.ShapeDtypeStruct((TP,) + ub.shape, BF),
+            jax.ShapeDtypeStruct((TP, HW, CW), BF),
+            jax.ShapeDtypeStruct((TP,) + vsend.shape, BF),
+        ),
+        in_specs=[VM, VM, ANY, VM],
+        out_specs=(ANY,) * 4,
+        scratch_shapes=[
+            pltpu.VMEM((HW, CW), BF),
+            DMA((2,)),
+            DMA((2,)),
+            DMA((5,)),
+            DMA((2, 4)),
+            DMA((2, 4)),
+            DMA((2, 4)),
+            DMA((2, 4)),
+            DMA((8,)),
+            DMA((8,)),
+            DMA((8,)),
+            DMA((8,)),
+            DMA((8,)),
+            DMA((8,)),
+        ],
+        compiler_params=comm_params(1),
+    )(xb, ub, wsend, vsend)
+
+
+def gather_kernel(y_ref, out, ls, sg, rg, sp, rp):
+    r, f, x, k, c, q, w = place()
+    partner = 2 * x + 1 - k
+    near_ids = [4 * c + flip(q, j) for j in range(1, 4)]
+    meet([(r, n) for n in near_ids] + [(partner, f)])
+    keep = pltpu.make_async_copy(y_ref, out.at[w], ls.at[0])
+    keep.start()
+    near = [
+        remote(y_ref, out.at[w], sg.at[j], rg.at[j], r, near_ids[j - 1]) for j in range(1, 4)
+    ]
+    for copy in near:
+        copy.start()
+    passed = [remote(y_ref, out.at[w], sp.at[0], rp.at[0], partner, f)]
+    passed[0].start()
+    for j in range(1, 4):
+        near[j - 1].wait_recv()
+        got = out.at[4 * k + flip(q, j)]
+        copy = remote(got, got, sp.at[j], rp.at[j], partner, f)
+        copy.start()
+        passed.append(copy)
+    for copy in near:
+        copy.wait_send()
+    for copy in passed:
+        copy.wait()
+    keep.wait()
+
+
+def gather_rows(y, cid):
+    return pl.pallas_call(
+        gather_kernel,
+        name="gather_rows",
+        out_shape=jax.ShapeDtypeStruct((TP,) + y.shape, y.dtype),
+        in_specs=[VM],
+        out_specs=ANY,
+        scratch_shapes=[DMA((1,))] + [DMA((4,))] * 4,
+        compiler_params=comm_params(cid),
+    )(y)
+
+
+def reduce_kernel(a_ref, w_ref, out, pair, got, small, far, sp, rp, sg, rg):
+    r, f, x, k, c, q, w = place()
+    partner = 2 * x + 1 - k
+    near_ids = [4 * c + flip(q, j) for j in range(4)]
+    meet([(r, n) for n in near_ids[1:]] + [(partner, f)])
+    order = (3, 2, 1, 0)
+    halves = []
+    for j in order:
+        pair[j] = contract_last(a_ref[4 * (1 - k) + flip(q, j)], w_ref[...])
+        copy = remote(pair.at[j], got.at[j], sp.at[j], rp.at[j], partner, f)
+        copy.start()
+        halves.append(copy)
+    sent = []
+    total = None
+    for n, j in enumerate(order):
+        part = contract_last(a_ref[4 * k + flip(q, j)], w_ref[...])
+        halves[n].wait_recv()
+        part = part + got[j]
+        if j:
+            small[j] = part.astype(BF)
+            copy = remote(small.at[j], far.at[j], sg.at[j], rg.at[j], r, near_ids[j])
+            copy.start()
+            sent.append(copy)
+        else:
+            total = part
+    for copy in sent:
+        copy.wait_recv()
+    for j in order[:-1]:
+        total = total + far[j].astype(F32)
+    out[...] = total
+    for copy in sent + halves:
+        copy.wait_send()
+
+
+def reduce_rows(a, weights, cid):
+    return pl.pallas_call(
+        reduce_kernel,
+        name="reduce_rows",
+        out_shape=jax.ShapeDtypeStruct((LEN, D), F32),
+        in_specs=[VM, VM],
+        out_specs=VM,
+        scratch_shapes=[
+            pltpu.VMEM((4, LEN, D), F32),
+            pltpu.VMEM((4, LEN, D), F32),
+            pltpu.VMEM((4, LEN, D), BF),
+            pltpu.VMEM((4, LEN, D), BF),
+        ]
+        + [DMA((4,))] * 4,
+        compiler_params=comm_params(cid),
+    )(a, weights)
+
+
+def first_head(shape):
+    return lax.broadcasted_iota(jnp.int32, shape, 1) < HD
+
+
+def attend_kernel(x_ref, m_ref, g_ref, s_ref, b_ref, w_ref, y_ref, qkv_ref, att_ref, p_ref):
+    normed, _, _ = normalize(x_ref[0].astype(F32), g_ref[...], s_ref[...])
+    y = normed.astype(BF)
+    y_ref[0] = y
+    qkv = (jnp.dot(y, w_ref[...], preferred_element_type=F32) + b_ref[...]).astype(BF)
+    qkv_ref[0] = qkv
+    queries, keys, values = qkv[:, :HW], qkv[:, HW : 2 * HW], qkv[:, 2 * HW :]
+    valid = m_ref[0, 0:1, :LEN].astype(F32) > 0.5
+    left = first_head(queries.shape)
+    sums = []
+    for h in range(2):
+        mine = left if h == 0 else jnp.logical_not(left)
+        part = jnp.where(mine, queries, jnp.zeros_like(queries))
+        scores = jnp.where(valid, contract_last(part, keys) * HD ** (-0.5), MASKED)
+        exponent = jnp.exp(scores - jnp.max(scores, axis=-1, keepdims=True))
+        probs = exponent / jnp.sum(exponent, axis=-1, keepdims=True)
+        p_ref[0, h] = probs
+        sums.append(jnp.dot(probs.astype(BF), values, preferred_element_type=F32))
+    att_ref[0] = jnp.where(left, sums[0], sums[1]).astype(BF)
+
+
+def attend(xf, uf, gain, shift, bias, weights):
+    row = lambda s: (s, 0, 0)
+    whole = lambda s: (0, 0)
+    return pl.pallas_call(
+        attend_kernel,
+        name="attend",
+        grid=(TP,),
+        out_shape=(
+            jax.ShapeDtypeStruct((TP, LEN, D), BF),
+            jax.ShapeDtypeStruct((TP, LEN, 3 * HW), BF),
+            jax.ShapeDtypeStruct((TP, LEN, HW), BF),
+            jax.ShapeDtypeStruct((TP, 2, LEN, LEN), F32),
+        ),
+        in_specs=[
+            pl.BlockSpec((1, LEN, D), row),
+            pl.BlockSpec((1, AUX, D), lambda s: (s, LEN // AUX, 0)),
+            pl.BlockSpec((1, D), whole),
+            pl.BlockSpec((1, D), whole),
+            pl.BlockSpec((1, 3 * HW), whole),
+            pl.BlockSpec((D, 3 * HW), whole),
+        ],
+        out_specs=(
+            pl.BlockSpec((1, LEN, D), row),
+            pl.BlockSpec((1, LEN, 3 * HW), row),
+            pl.BlockSpec((1, LEN, HW), row),
+            pl.BlockSpec((1, 2, LEN, LEN), lambda s: (s, 0, 0, 0)),
+        ),
+    )(xf, uf, gain, shift, bias, weights)
+
+
+def attend_back_kernel(m_ref, wo_ref, qkv_ref, p_ref, out):
+    grad = jnp.dot(m_ref[0], wo_ref[...], preferred_element_type=F32).astype(BF)
+    qkv = qkv_ref[0]
+    queries, keys, values = qkv[:, :HW], qkv[:, HW : 2 * HW], qkv[:, 2 * HW :]
+    left = first_head(queries.shape)
+    gq, gk, gv = [], [], []
+    for h in range(2):
+        mine = left if h == 0 else jnp.logical_not(left)
+        part = jnp.where(mine, grad, jnp.zeros_like(grad))
+        probs = p_ref[0, h]
+        grad_probs = contract_last(part, values)
+        row_dot = jnp.sum(probs * grad_probs, axis=-1, keepdims=True)
+        grad_scores = (probs * (grad_probs - row_dot)).astype(BF)
+        gq.append(jnp.dot(grad_scores, keys, preferred_element_type=F32))
+        gk.append(contract_rows(grad_scores, queries))
+        gv.append(contract_rows(probs.astype(BF), grad))
+    scale = HD ** (-0.5)
+    out[0, :, :HW] = (jnp.where(left, gq[0], gq[1]) * scale).astype(BF)
+    out[0, :, HW : 2 * HW] = (jnp.where(left, gk[0], gk[1]) * scale).astype(BF)
+    out[0, :, 2 * HW :] = jnp.where(left, gv[0], gv[1]).astype(BF)
+
+
+def attend_back(middle, weights, qkv, probs):
+    row = lambda s: (s, 0, 0)
+    return pl.pallas_call(
+        attend_back_kernel,
+        name="attend_back",
+        grid=(TP,),
+        out_shape=jax.ShapeDtypeStruct((TP, LEN, 3 * HW), BF),
+        in_specs=[
+            pl.BlockSpec((1, LEN, D), row),
+            pl.BlockSpec((D, HW), lambda s: (0, 0)),
+            pl.BlockSpec((1, LEN, 3 * HW), row),
+            pl.BlockSpec((1, 2, LEN, LEN), lambda s: (s, 0, 0, 0)),
+        ],
+        out_specs=pl.BlockSpec((1, LEN, 3 * HW), row),
+    )(middle, weights, qkv, probs)
+
+
+def units_kernel(y_ref, u_ref, up_ref, down_ref, b_ref, act_ref, grad_ref):
+    pre = jnp.dot(y_ref[0], up_ref[...], preferred_element_type=F32) + b_ref[...]
+    grad_act = jnp.dot(u_ref[0], down_ref[...], preferred_element_type=F32)
+    below = 0.5 * (1.0 + lax.erf(pre * (0.5**0.5)))
+    density = jnp.exp(-0.5 * pre * pre) * 0.3989422804014327
+    act_ref[0] = (pre * below).astype(BF)
+    grad_ref[0] = (grad_act * (below + pre * density)).astype(BF)
+
+
+def units(y, uf, up, down, bias):
+    row = lambda s: (s, 0, 0)
+    whole = lambda s: (0, 0)
+    return pl.pallas_call(
+        units_kernel,
+        name="units",
+        grid=(TP,),
+        out_shape=(jax.ShapeDtypeStruct((TP, LEN, FW), BF),) * 2,
+        in_specs=[
+            pl.BlockSpec((1, LEN, D), row),
+            pl.BlockSpec((1, LEN, D), row),
+            pl.BlockSpec((D, FW), whole),
+            pl.BlockSpec((D, FW), whole),
+            pl.BlockSpec((1, FW), whole),
+        ],
+        out_specs=(pl.BlockSpec((1, LEN, FW), row),) * 2,
+    )(y, uf, up, down, bias)
+
+
+def weight_grads_kernel(y1, mid, y2, up, gq, att, gp, act, out):
+    flat = lambda ref: ref[...].reshape(TP * LEN, ref.shape[-1])
+    out[:, : 3 * HW] = contract_rows(flat(y1), flat(gq)).astype(BF)
+    out[:, 3 * HW : 4 * HW] = contract_rows(flat(mid), flat(att)).astype(BF)
+    out[:, 4 * HW : 4 * HW + FW] = contract_rows(flat(y2), flat(gp)).astype(BF)
+    out[:, 4 * HW + FW :] = contract_rows(flat(up), flat(act)).astype(BF)
+
+
+def weight_grads(y1, mid, y2, uf, gq, att, gp, act):
+    step = 256
+    left = pl.BlockSpec((TP, LEN, step), lambda i: (0, 0, i))
+    right = lambda n: pl.BlockSpec((TP, LEN, n), lambda i: (0, 0, 0))
+    return pl.pallas_call(
+        weight_grads_kernel,
+        name="weight_grads",
+        grid=(D // step,),
+        out_shape=jax.ShapeDtypeStruct((D, CW), BF),
+        in_specs=[left] * 4 + [right(3 * HW), right(HW), right(FW), right(FW)],
+        out_specs=pl.BlockSpec((step, CW), lambda i: (i, 0)),
+    )(y1, mid, y2, uf, gq, att, gp, act)
+
+
+def return_kernel(g_ref, v_ref, b_ref, i_ref, gr, vr, bo, io, own, ls, sw, rw, sg, rg, sv, rv):
+    r, f, x, k, c, q, w = place()
+    meet([(2 * x + (k + kk) % 2, (f + i) % 8) for kk in range(2) for i in range(8) if kk or i])
+    home = 2 * x + c
+    pf = 4 * k + q
+    swaps = [remote(b_ref, bo, sw.at[0], rw.at[0], home, pf), remote(i_ref, io, sw.at[1], rw.at[1], home, pf)]
+    keeps = [pltpu.make_async_copy(b_ref, bo, ls.at[0]), pltpu.make_async_copy(i_ref, io, ls.at[1])]
+    load = pltpu.make_async_copy(g_ref.at[f], own, ls.at[2])
+    keep_own = pltpu.make_async_copy(own, gr.at[w], ls.at[3])
+    keep_vec = pltpu.make_async_copy(v_ref.at[f], vr.at[w], ls.at[4])
+
+    def blocks(i):
+        to = (f + i) % 8
+        return (
+            remote(v_ref.at[to], vr.at[w], sv.at[i], rv.at[w], home, to),
+            remote(g_ref.at[to], gr.at[w], sg.at[i], rg.at[w], home, to),
+        )
+
+    for i in range(1, 8):
+        for copy in blocks(i):
+            copy.start()
+
+    @pl.when(k != c)
+    def _():
+        for copy in blocks(0):
+            copy.start()
+        for copy in swaps:
+            copy.start()
+
+    @pl.when(k == c)
+    def _():
+        for copy in keeps + [load, keep_vec]:
+            copy.start()
+        load.wait()
+        keep_own.start()
+
+    for kk in range(2):
+        for p in range(4):
+            source = 4 * kk + p
+
+            def landed():
+                remote(v_ref.at[0], vr.at[source], sv.at[0], rv.at[source], r, f).wait_recv()
+                remote(g_ref.at[0], gr.at[source], sg.at[0], rg.at[source], r, f).wait_recv()
+
+            @pl.when(jnp.logical_or(c != k, source != w))
+            def _(landed=landed):
+                landed()
+
+    for i in range(1, 8):
+        for copy in blocks(i):
+            copy.wait_send()
+
+    @pl.when(k != c)
+    def _():
+        for copy in blocks(0):
+            copy.wait_send()
+        for copy in swaps:
+            copy.wait()
+
+    @pl.when(k == c)
+    def _():
+        for copy in keeps + [keep_vec, keep_own]:
+            copy.wait()
+
+
+def return_exchange(grads, vecs, block, grad_in):
+    shape = lambda a: jax.ShapeDtypeStruct(a.shape, a.dtype)
+    return pl.pallas_call(
+        return_kernel,
+        name="return_exchange",
+        out_shape=tuple(shape(a) for a in (grads, vecs, block, grad_in)),
+        in_specs=[ANY, VM, VM, VM],
+        out_specs=(ANY, VM, ANY, ANY),
+        scratch_shapes=[pltpu.VMEM(grads.shape[1:], BF), DMA((5,)), DMA((2,)), DMA((2,))] + [DMA((8,))] * 4,
+        compiler_params=comm_params(8),
+    )(grads, vecs, block, grad_in)
+
+
+def pieces():
+    return [(n * HW, HW) for n in range(4)], [(4 * HW + n * FW, FW) for n in range(2)]
+
+
+def adam_kernel(g_ref, wa, wf, ma, mf, nv, ga, gf, gw, da, df):
+    narrow, wide = pieces()
+    for parts, master, moments, grads, delta, at in (
+        (narrow, wa, ma, ga, da, 0),
+        (wide, wf, mf, gf, df, 4 * D),
+    ):
+        for n, (start, width) in enumerate(parts):
+            for s in range(TP):
+                grads[0, :, n * TP * width + s * width : n * TP * width + (s + 1) * width] = g_ref[
+                    s, :, start : start + width
+                ].astype(F32)
+        weight = master[0]
+        new, first, second = adamw_step(weight, grads[0], (moments[0, 0], moments[0, 1]), ADAM_DECAY)
+        grads[1] = first
+        grads[2] = second
+        gw[:, at : at + weight.shape[1]] = new
+        delta[...] = (new - weight).astype(BF)
+    gw[:, 4 * D + 2 * FF :] = nv[...]
+
+
+def adam(grads, outer_attention, outer_feedforward, moments_attention, moments_feedforward, new_vectors):
+    step = 16
+    na, nf = 4 * D, 2 * FF
+    rows3 = lambda i: (0, i, 0)
+    rows2 = lambda i: (i, 0)
+    return pl.pallas_call(
+        adam_kernel,
+        name="adam",
+        grid=(HW // step,),
+        out_shape=(
+            jax.ShapeDtypeStruct((3, HW, na), F32),
+            jax.ShapeDtypeStruct((3, HW, nf), F32),
+            jax.ShapeDtypeStruct((HW, na + nf + 12), F32),
+            jax.ShapeDtypeStruct((HW, na), BF),
+            jax.ShapeDtypeStruct((HW, nf), BF),
+        ),
+        in_specs=[
+            pl.BlockSpec((TP, step, CW), rows3),
+            pl.BlockSpec((1, step, na), rows3),
+            pl.BlockSpec((1, step, nf), rows3),
+            pl.BlockSpec((1, 2, step, na), lambda i: (0, 0, i, 0)),
+            pl.BlockSpec((1, 2, step, nf), lambda i: (0, 0, i, 0)),
+            pl.BlockSpec((step, 12), rows2),
+        ],
+        out_specs=(
+            pl.BlockSpec((3, step, na), rows3),
+            pl.BlockSpec((3, step, nf), rows3),
+            pl.BlockSpec((step, na + nf + 12), rows2),
+            pl.BlockSpec((step, na), rows2),
+            pl.BlockSpec((step, nf), rows2),
+        ),
+    )(grads, outer_attention, outer_feedforward, moments_attention, moments_feedforward, new_vectors)
+
+
+def groups_kernel(a_ref, f_ref, v_ref, pa, pf, qa, qf, vo, ba, bf_, vb, ss, rs, sx, rx, sf, rf, sv, rv):
+    r, f, x, k, c, q, w = place()
+    partner, across = 2 * x + 1 - k, 2 * (1 - x) + k
+    meet([(partner, f), (across, f)])
+    rows = 16
+    count = HW // 2 // rows
+    mine = lambda half, j: pl.ds(pl.multiple_of(half * (HW // 2) + j * rows, rows), rows)
+    trio = ((a_ref, ba, pa, qa), (f_ref, bf_, pf, qf))
+    vec = remote(v_ref, vb.at[0], sv.at[0], rv.at[0], partner, f)
+    vec.start()
+    first = {}
+    for turn in range(2):
+        half = (1 - k) if turn == 0 else k
+        for j in range(count):
+            for n, (src, buf, _, _) in enumerate(trio):
+                copy = remote(src.at[mine(half, j)], buf.at[mine(half, j)], ss.at[turn, n, j], rs.at[turn, n, j], partner, f)
+                copy.start()
+                first[turn, n, j] = copy
+    vec.wait_recv()
+    vb[1] = v_ref[...] + vb[0]
+    vec2 = remote(vb.at[1], vb.at[2], sv.at[1], rv.at[1], across, f)
+    vec2.start()
+    second = {}
+    for turn in range(2):
+        half = k if turn == 0 else 1 - k
+        for j in range(count):
+            for n, (src, buf, pair, other) in enumerate(trio):
+                first[turn, n, j].wait_recv()
+                at = mine(half, j)
+                pair[at, :] = (src[at, :].astype(F32) + buf[at, :].astype(F32)).astype(BF)
+                if turn == 0:
+                    copy = remote(pair.at[at], other.at[at], sx.at[n, j], rx.at[n, j], across, f)
+                    copy.start()
+                    second[n, j] = copy
+    third = []
+    for j in range(count):
+        for n, (_, _, _, other) in enumerate(trio):
+            second[n, j].wait_recv()
+            at = mine(k, j)
+            copy = remote(other.at[at], other.at[at], sf.at[n, j], rf.at[n, j], partner, f)
+            copy.start()
+            third.append(copy)
+    vec2.wait_recv()
+    vo[...] = vb[1] + vb[2]
+    for copy in third:
+        copy.wait()
+    for copy in list(first.values()) + list(second.values()) + [vec, vec2]:
+        copy.wait_send()
+
+
+def groups_sum(delta_a, delta_f, delta_v):
+    count = HW // 2 // 16
+    sa, sf, sv = (jax.ShapeDtypeStruct(a.shape, a.dtype) for a in (delta_a, delta_f, delta_v))
+    return pl.pallas_call(
+        groups_kernel,
+        name="groups_sum",
+        out_shape=(sa, sf, sa, sf, sv),
+        in_specs=[VM] * 3,
+        out_specs=(VM,) * 5,
+        scratch_shapes=[
+            pltpu.VMEM(delta_a.shape, BF),
+            pltpu.VMEM(delta_f.shape, BF),
+            pltpu.VMEM((3,) + delta_v.shape, F32),
+            DMA((2, 2, count)),
+            DMA((2, 2, count)),
+            DMA((2, count)),
+            DMA((2, count)),
+            DMA((2, count)),
+            DMA((2, count)),
+            DMA((2,)),
+            DMA((2,)),
+        ],
+        compiler_params=comm_params(9),
+    )(delta_a, delta_f, delta_v)
+
+
+def outer_kernel(pa, pf, qa, qf, oa, of, na, nf, ca, cf):
+    for pair, other, outer, out, copy in ((pa, qa, oa, na, ca), (pf, qf, of, nf, cf)):
+        mean = (pair[...].astype(F32) + other[...].astype(F32)) / 4
+        momentum = OUTER_MOMENTUM * outer[1] - mean
+        following = outer[0] - OUTER_RATE * (OUTER_MOMENTUM * momentum - mean)
+        out[0] = mean
+        out[1] = momentum
+        out[2] = following
+        copy[...] = following.astype(BF)
+
+
+def outer_update(pa, pf, qa, qf, outer_attention, outer_feedforward):
+    step = 16
+    na, nf = 4 * D, 2 * FF
+    rows2 = lambda i: (i, 0)
+    rows3 = lambda i: (0, i, 0)
+    two = [pl.BlockSpec((step, n), rows2) for n in (na, nf)]
+    return pl.pallas_call(
+        outer_kernel,
+        name="outer_update",
+        grid=(HW // step,),
+        out_shape=(
+            jax.ShapeDtypeStruct((3, HW, na), F32),
+            jax.ShapeDtypeStruct((3, HW, nf), F32),
+            jax.ShapeDtypeStruct((HW, na), BF),
+            jax.ShapeDtypeStruct((HW, nf), BF),
+        ),
+        in_specs=two + two + [pl.BlockSpec((2, step, n), rows3) for n in (na, nf)],
+        out_specs=tuple([pl.BlockSpec((3, step, n), rows3) for n in (na, nf)] + two),
+    )(pa, pf, qa, qf, outer_attention, outer_feedforward)
+
+
+def shards_split(
+    features,
+    cotangent,
+    clip_lengths,
+    group_clips,
+    outer_attention,
+    outer_feedforward,
+    outer_vectors,
+    moments_attention,
+    moments_feedforward,
+    moments_vectors,
+):
+    r, f, x, k, c, q, w = place()
+    clip_length = lax.dynamic_index_in_dim(clip_lengths[0], f, keepdims=False)
+    positions = jnp.arange(LEN, dtype=jnp.int32)
+    key_valid = positions < clip_length
+    row_valid = key_valid & (f < group_clips[0])
+    up_here = jnp.where(row_valid[:, None], cotangent, jnp.zeros_like(cotangent))
+    flags = jnp.broadcast_to(jnp.pad(key_valid.astype(BF), (0, D - LEN))[None], (AUX, D))
+    ub = jnp.concatenate([up_here, flags], axis=0)
+    part_a = outer_attention[0].astype(BF).reshape(HW, 4, 2, 4, HW)
+    part_f = outer_feedforward[0].astype(BF).reshape(HW, 2, 2, 4, FW)
+    part_a = lax.dynamic_index_in_dim(part_a, k, 2, keepdims=False).transpose(2, 0, 1, 3)
+    part_f = lax.dynamic_index_in_dim(part_f, k, 2, keepdims=False).transpose(2, 0, 1, 3)
+    wsend = jnp.concatenate([part_a.reshape(4, HW, 4 * HW), part_f.reshape(4, HW, 2 * FW)], axis=2)
+    vsend = jnp.pad(outer_vectors[0].astype(BF), ((0, 4), (0, 96)))
+    xf, uf, wf, vf = first_exchange(features, ub, wsend, vsend)
+    vectors = vf[:, :12, :HW].transpose(1, 0, 2).reshape(12, D).astype(F32)
+    columns = wf.reshape(D, CW)
+    w_qkv, w_out = columns[:, : 3 * HW], columns[:, 3 * HW : 4 * HW]
+    w_up, w_down = columns[:, 4 * HW : 4 * HW + FW], columns[:, 4 * HW + FW :]
+    own = lambda row, width: lax.dynamic_slice_in_dim(row, w * width, width, 0)
+    bias_qkv = jnp.concatenate([own(vectors[2], HW), jnp.zeros((HW,), F32), own(vectors[3], HW)])[None]
+    bias_up = own(vectors[8:].reshape(FF), FW)[None]
+    x_own = lax.dynamic_index_in_dim(xf, w, keepdims=False).astype(F32)
+    up_own = lax.dynamic_index_in_dim(uf, w, keepdims=False)[:LEN]
+    upstream = up_own.astype(F32)
+    _, unit_one, scale_one = normalize(x_own, vectors[0], vectors[1])
+
+    y1, qkv, attended, probs = attend(xf, uf, vectors[0:1], vectors[1:2], bias_qkv, w_qkv)
+    middle = x_own + (reduce_rows(attended, w_out, 2) + vectors[4])
+    normed_two, unit_two, scale_two = normalize(middle, vectors[5], vectors[6])
+    y2 = gather_rows(normed_two.astype(BF), 3)
+    act, grad_pre = units(y2, uf, w_up, w_down, bias_up)
+    block_output = (middle + (reduce_rows(act, w_down, 4) + vectors[7])).astype(BF)
+    grad_two = reduce_rows(grad_pre, w_up, 5)
+    grad_middle = upstream + normalize_back(grad_two, unit_two, scale_two, vectors[5])
+    middle_low = grad_middle.astype(BF)
+    mid = gather_rows(middle_low, 6)
+    grad_qkv = attend_back(mid, w_out, qkv, probs)
+    grad_one = reduce_rows(grad_qkv, w_qkv, 7)
+    input_grad = grad_middle + normalize_back(grad_one, unit_one, scale_one, vectors[0])
+    grads = weight_grads(y1, mid, y2, uf, grad_qkv, attended, grad_pre, act).reshape(TP, HW, CW)
+
+    total = lambda a: jnp.sum(a, axis=0, dtype=F32)
+    sums_qkv = total(grad_qkv.reshape(TP * LEN, 3 * HW))
+    spread = lambda part, size: lax.dynamic_update_slice_in_dim(
+        jnp.zeros((size,), F32), part, w * part.shape[0], 0
+    )
+    rows = jnp.stack(
+        [
+            total(grad_one * unit_one),
+            total(grad_one),
+            spread(sums_qkv[:HW], D),
+            spread(sums_qkv[2 * HW :], D),
+            total(middle_low),
+            total(grad_two * unit_two),
+            total(grad_two),
+            total(up_own),
+        ]
+    )
+    partial_vectors = jnp.concatenate(
+        [rows, spread(total(grad_pre.reshape(TP * LEN, FW)), FF).reshape(4, D)], axis=0
+    )
+    vec_send = jnp.pad(partial_vectors.reshape(12, TP, HW).transpose(1, 0, 2), ((0, 0), (0, 4), (0, 96)))
+    grads_in, vecs_in, block_home, grad_home = return_exchange(grads, vec_send, block_output, input_grad)
+    owned_vectors = jnp.sum(vecs_in, axis=0)[:12, :HW]
+    new_vectors, first_vectors, second_vectors = adamw_step(
+        outer_vectors[0], owned_vectors, moments_vectors[0], 0.0
+    )
+    group_a, group_f, group_w, delta_a, delta_f = adam(
+        grads_in, outer_attention, outer_feedforward, moments_attention, moments_feedforward, new_vectors.T
+    )
+    delta_v = jnp.pad(new_vectors - outer_vectors[0], ((0, 4), (0, 96)))
+    pa, pf, qa, qf, sum_v = groups_sum(delta_a, delta_f, delta_v)
+    next_a, next_f, copy_a, copy_f = outer_update(pa, pf, qa, qf, outer_attention, outer_feedforward)
+    next_v = outer_step(outer_vectors[0], sum_v[:12, :HW] / 4, outer_vectors[1])
+    return (
+        block_home,
+        grad_home,
+        group_a[None],
+        group_f[None],
+        jnp.stack([owned_vectors, first_vectors, second_vectors])[None],
+        group_w[None],
+        next_a,
+        next_f,
+        next_v,
+        copy_a,
+        copy_f,
+        next_v[2].astype(BF),
+    )
+
+
 def solution(mesh):
+    shape = dict(mesh.shape)
+    fits = shape == {"rep": 4, "fsdp": 8}
+    shards = shards_split if fits else shards_generic
     in_specs = (
         P(("rep", "fsdp"), None),
         P(("rep", "fsdp"), None),

time: 2360 us -> 639 us (0.27)
  waiting for transfers between devices: 2000 us -> 0 us
  Pallas kernels: 0 us -> 573 us
  other arithmetic: 120 us -> 22.2 us
  matrix products: 91.1 us -> 0 us
  blocking collectives: 51.4 us -> 0 us
  local copies, waits for them, and re-layouts: 74.4 us -> 40.2 us
    reduce_scatter x5 -> x0, waiting for transfers between devices: 1230 us -> none  [the longest x1 811 us: shards(): lax.psum_scatter(jnp.concatenate([contract_rows(layer_two, grad_pre), con...]
    all_gather x4 -> x0, waiting for transfers between devices: 764 us -> none  [the longest x1 489 us: shards(): lax.all_gather(copies[1], 'fsdp', axis=0, tiled=True)]
    pallas_call x0 -> x15, Pallas kernels: none -> 573 us  [the longest x1 136 us: first_exchange(): pl.pallas_call(first_kernel, name='first_exchange', out_shape=(jax.ShapeD...]
    dot_general x18 -> x0, matrix products: 91.1 us -> none  [the longest x4 31 us: contract_last(): lax.dot_general(left, right, (((1,), (1,)), ((), ())), preferred_element_...]
    concatenate x3, other arithmetic: 44.9 us -> 4.2 us  [the longest x1 2.78 us: shards_split(): jnp.concatenate([part_a.reshape(4, HW, 4 * HW), part_f.reshape(4, HW, 2 *...]
    all_gather x2 -> x0, blocking collectives: 39.4 us -> none  [the longest x1 33.6 us: shards(): lax.all_gather(copies[2], 'fsdp', axis=1, tiled=True)]
    broadcast_in_dim x4 -> x1, other arithmetic: 32.8 us -> 0.01 us  [shards_split(): jnp.stack([owned_vectors, first_vectors, second_vectors])[None]]
    convert_element_type x6 -> x3, other arithmetic: 30.5 us -> 2.38 us  [the longest x1 0.92 us: shards_split(): y2 = gather_rows(normed_two.astype(BF), 3)]
  transfers between devices with their start and end apart: 9 -> 0, of which waited for: 8 -> 0; matrix products, arithmetic and copies ran while one was open for 9% -> 0% of each run, Pallas kernels for 0% -> 0%
where the time goes in v1:
time: 639 us; the launch traced here: 638 us
  Pallas kernels  573 us (90%)
  local copies, waits for them, and re-layouts  40.2 us (6%)
  other arithmetic  22.2 us (3%)
    pallas_call x1, Pallas kernels, first_exchange(): pl.pallas_call(first_kernel, name='first_exchange', out_shape=(jax.ShapeD...  136 us
    pallas_call x1, Pallas kernels, groups_sum(): pl.pallas_call(groups_kernel, name='groups_sum', out_shape=(sa, sf, sa, s...  114 us
    pallas_call x4, Pallas kernels, reduce_rows(): pl.pallas_call(reduce_kernel, name='reduce_rows', out_shape=jax.ShapeDtyp...  96.1 us
    pallas_call x1, Pallas kernels, return_exchange(): pl.pallas_call(return_kernel, name='return_exchange', out_shape=tuple((sh...  86.8 us
    pallas_call x2, Pallas kernels, gather_rows(): pl.pallas_call(gather_kernel, name='gather_rows', out_shape=jax.ShapeDtyp...  40.9 us
    pallas_call x1, Pallas kernels, adam(): pl.pallas_call(adam_kernel, name='adam', grid=(HW // step,), out_shape=(j...  31.6 us
    pallas_call x1, Pallas kernels, outer_update(): pl.pallas_call(outer_kernel, name='outer_update', grid=(HW // step,), out...  23.5 us

profile of v1, /device:TPU:0, one launch (start us, length us, event | category | flops | bytes accessed | tf_op | source)
XLA Modules:
  0.0 637.5 jit_solution(3663154972252495109)
XLA Ops:
  2.6 1.1 broadcast_select_fusion
  3.7 0.8 pad_maximum_fusion.1.u_ref
  4.4 3.2 slice.184
  7.7 4.0 convert_element_type.66
  11.7 2.0 constant_dynamic-slice_fusion.2
  13.7 1.3 copy.101
  14.9 1.1 reshape.150
  16.0 2.1 slice.185
  18.2 3.9 convert_element_type.65
  22.1 1.8 constant_dynamic-slice_fusion.3
  24.4 1.6 reshape.149
  26.0 2.8 pad_maximum_fusion.w_ref
  29.4 136.2 %first_exchange.1 = (bf16[8,128,1280]{2,1,0:T(8,128)(2,1)}, bf16[8,144,1280]{2,1,0:T(8,128)(2,1)}, bf16[8,160,1920]{2,1,0:T(8,128)(2,1)}, bf16[8,16,256]{2,1,0:T(8,128)(2,1)}) custom-call(bf16[128,1280]{1,0:T(8,128)(2,1)} %x_ref.1, bf16[144,1280]{1,0:T(8,128)(2,1)} %pad_maximum_fusion.1.u_ref, bf16[4,160,1920]{2,1,0:T(8,128)(2,1)} %pad_maximum_fusion.w_ref, ...), custom_call_target="tpu_custom_call" | custom-call | tf_op jit(solution)/shard_map/first_exchange/pallas_call | solution.py:456
  165.6 0.9 convert_bitcast_fusion.2
  166.7 0.7 slice.107.g_ref
  167.3 0.7 slice.109.s_ref
  168.3 0.7 pad_maximum_fusion.3
  169.0 2.5 slice.137.w_ref
  171.4 11.7 %attend.1 = (bf16[8,128,1280]{2,1,0:T(8,128)(2,1)}, bf16[8,128,480]{2,1,0:T(8,128)(2,1)}, bf16[8,128,160]{2,1,0:T(8,128)(2,1)}, f32[8,2,128,128]{3,2,1,0:T(8,128)}) custom-call(bf16[8,128,1280]{2,1,0:T(8,128)(2,1)} %get-tuple-element.40.x_ref, bf16[8,144,1280]{2,1,0:T(8,128)(2,1)} %get-tuple-element.41.m_ref.u_ref.up, f32[1,1280]{1,0:T(1,128)} %slice.107.g_ref, ...), custom_call_target="tpu_custom_call" | custom-call | tf_op jit(solution)/shard_map/attend/pallas_call | solution.py:606
  183.1 2.3 slice.138.w_ref.wo_ref
  185.4 22.9 %reduce_rows.4 = f32[128,1280]{1,0:T(8,128)} custom-call(bf16[8,128,160]{2,1,0:T(8,128)(2,1)} %get-tuple-element.45.a_ref.att, bf16[1280,160]{1,0:T(8,128)(2,1)} %slice.138.w_ref.wo_ref), custom_call_target="tpu_custom_call" | custom-call | tf_op jit(solution)/shard_map/reduce_rows/pallas_call | solution.py:561
  208.4 1.1 convert_reduce_fusion.2
  209.5 1.4 fusion.34
  211.3 0.9 add_convert_fusion.1.y_ref
  212.2 20.5 %gather_rows.2.y_ref.y2 = bf16[8,128,1280]{2,1,0:T(8,128)(2,1)} custom-call(bf16[128,1280]{1,0:T(8,128)(2,1)} %add_convert_fusion.1.y_ref), custom_call_target="tpu_custom_call" | custom-call | tf_op jit(solution)/shard_map/gather_rows/pallas_call | solution.py:515
  232.7 3.9 fusion.36
  237.4 9.9 %units.1 = (bf16[8,128,640]{2,1,0:T(8,128)(2,1)}, bf16[8,128,640]{2,1,0:T(8,128)(2,1)}) custom-call(bf16[8,128,1280]{2,1,0:T(8,128)(2,1)} %gather_rows.2.y_ref.y2, bf16[8,144,1280]{2,1,0:T(8,128)(2,1)} %get-tuple-element.41.m_ref.u_ref.up, bf16[1280,640]{1,0:T(8,128)(2,1)} %get-tuple-element.116.up_ref.w_ref, ...), custom_call_target="tpu_custom_call" | custom-call | tf_op jit(solution)/shard_map/units/pallas_call | solution.py:684
  247.3 24.7 %reduce_rows.5 = f32[128,1280]{1,0:T(8,128)} custom-call(bf16[8,128,640]{2,1,0:T(8,128)(2,1)} %get-tuple-element.46.a_ref.gp, bf16[1280,640]{1,0:T(8,128)(2,1)} %get-tuple-element.116.up_ref.w_ref), custom_call_target="tpu_custom_call" | custom-call | tf_op jit(solution)/shard_map/reduce_rows/pallas_call | solution.py:561
  272.0 24.5 %reduce_rows.7 = f32[128,1280]{1,0:T(8,128)} custom-call(bf16[8,128,640]{2,1,0:T(8,128)(2,1)} %get-tuple-element.49.act.a_ref, bf16[1280,640]{1,0:T(8,128)(2,1)} %get-tuple-element.115.down_ref.w_ref), custom_call_target="tpu_custom_call" | custom-call | tf_op jit(solution)/shard_map/reduce_rows/pallas_call | solution.py:561
  296.5 2.1 multiply_reduce_fusion
  298.6 2.2 convert_reduce_fusion.4
  300.9 20.4 %gather_rows.3.m_ref.mid = bf16[8,128,1280]{2,1,0:T(8,128)(2,1)} custom-call(bf16[128,1280]{1,0:T(8,128)(2,1)} %get-tuple-element.111.y_ref), custom_call_target="tpu_custom_call" | custom-call | tf_op jit(solution)/shard_map/gather_rows/pallas_call | solution.py:515
  321.3 11.2 %attend_back.1.gq.a_ref = bf16[8,128,480]{2,1,0:T(8,128)(2,1)} custom-call(bf16[8,128,1280]{2,1,0:T(8,128)(2,1)} %gather_rows.3.m_ref.mid, bf16[1280,160]{1,0:T(8,128)(2,1)} %slice.138.w_ref.wo_ref, bf16[8,128,480]{2,1,0:T(8,128)(2,1)} %get-tuple-element.47.qkv_ref, f32[8,2,128,128]{3,2,1,0:T(8,128)} %get-tuple-element.48.p_ref), custom_call_target="tpu_custom_call" | custom-call | tf_op jit(solution)/shard_map/attend_back/pallas_call | solution.py:657
  332.5 12.0 %weight_grads.1 = bf16[1280,1920]{1,0:T(8,128)(2,1)} custom-call(bf16[8,128,1280]{2,1,0:T(8,128)(2,1)} %get-tuple-element.44.y1, bf16[8,128,1280]{2,1,0:T(8,128)(2,1)} %gather_rows.3.m_ref.mid, bf16[8,128,1280]{2,1,0:T(8,128)(2,1)} %gather_rows.2.y_ref.y2, bf16[8,144,1280]{2,1,0:T(8,128)(2,1)} %get-tuple-element.41.m_ref.u_ref.up, ...), custom_call_target="tpu_custom_call" | custom-call | tf_op jit(solution)/shard_map/weight_grads/pallas_call | solution.py:712
  344.5 24.1 %reduce_rows.6 = f32[128,1280]{1,0:T(8,128)} custom-call(bf16[8,128,480]{2,1,0:T(8,128)(2,1)} %attend_back.1.gq.a_ref, bf16[1280,480]{1,0:T(8,128)(2,1)} %slice.137.w_ref), custom_call_target="tpu_custom_call" | custom-call | tf_op jit(solution)/shard_map/reduce_rows/pallas_call | solution.py:561
  368.7 1.5 fusion.8
  371.5 1.0 convert_reduce_fusion.3
  373.4 0.7 pad.22.v_ref
  374.1 2.1 fusion.11.i_ref
  376.2 86.8 %return_exchange.1 = (bf16[8,160,1920]{2,1,0:T(8,128)(2,1)}, f32[8,16,256]{2,1,0:T(8,128)}, bf16[128,1280]{1,0:T(8,128)(2,1)}, f32[128,1280]{1,0:T(8,128)}) custom-call(bf16[8,160,1920]{2,1,0:T(8,128)(2,1)} %bitcast.129, f32[8,16,256]{2,1,0:T(8,128)} %pad.22.v_ref, bf16[128,1280]{1,0:T(8,128)(2,1)} %get-tuple-element.118.b_ref, f32[128,1280]{1,0:T(8,128)} %fusion.11.i_ref), custom_call_target="tpu_custom_call" | custom-call | tf_op jit(solution)/shard_map/return_exchange/pallas_call | solution.py:789
  463.0 0.9 reduce_sum.169
  464.0 0.7 copy.37.nv
  464.7 31.6 %adam.1 = (f32[3,160,5120]{2,1,0:T(8,128)}, f32[3,160,10240]{2,1,0:T(8,128)}, f32[160,15372]{1,0:T(8,128)}, bf16[160,5120]{1,0:T(8,128)(2,1)}, bf16[160,10240]{1,0:T(8,128)(2,1)}) custom-call(bf16[8,160,1920]{2,1,0:T(8,128)(2,1)} %get-tuple-element.52.g_ref, f32[2,160,5120]{2,1,0:T(8,128)} %oa.1, f32[2,160,10240]{2,1,0:T(8,128)} %of.1, ...), custom_call_target="tpu_custom_call" | custom-call | tf_op jit(solution)/shard_map/adam/pallas_call | solution.py:829
  496.3 0.7 copy.39
  497.6 113.6 %groups_sum.1 = (bf16[160,5120]{1,0:T(8,128)(2,1)}, bf16[160,10240]{1,0:T(8,128)(2,1)}, bf16[160,5120]{1,0:T(8,128)(2,1)}, bf16[160,10240]{1,0:T(8,128)(2,1)}, f32[16,256]{1,0:T(8,128)}) custom-call(bf16[160,5120]{1,0:T(8,128)(2,1)} %get-tuple-element.57.a_ref, bf16[160,10240]{1,0:T(8,128)(2,1)} %get-tuple-element.58.f_ref, f32[16,256]{1,0:T(8,128)} %pad.23.v_ref), custom_call_target="tpu_custom_call" | custom-call | tf_op jit(solution)/shard_map/groups_sum/pallas_call | solution.py:911
  611.2 23.5 %outer_update.1 = (f32[3,160,5120]{2,1,0:T(8,128)}, f32[3,160,10240]{2,1,0:T(8,128)}, bf16[160,5120]{1,0:T(8,128)(2,1)}, bf16[160,10240]{1,0:T(8,128)(2,1)}) custom-call(bf16[160,5120]{1,0:T(8,128)(2,1)} %get-tuple-element.59.pa, bf16[160,10240]{1,0:T(8,128)(2,1)} %get-tuple-element.60.pf, bf16[160,5120]{1,0:T(8,128)(2,1)} %get-tuple-element.61.qa, ...), custom_call_target="tpu_custom_call" | custom-call | tf_op jit(solution)/shard_map/outer_update/pallas_call | solution.py:951
  636.0 0.7 copy.113
  636.7 0.8 copy.114
  (85 shorter events, 8.3 us)
Async XLA Ops:
  0.6 0.7 copy-start
  26.0 2.8 copy-start.9
  271.9 24.6 %copy-start.5 = (f32[128,1280]{1,0:T(8,128)S(1)}, f32[128,1280]{1,0:T(8,128)}, u32[]{:S(2)}) copy-start(f32[128,1280]{1,0:T(8,128)} %reduce_rows.5) | copy-start | bytes 1966084
  344.5 25.9 %copy-start.2 = (bf16[8,128,480]{2,1,0:T(8,128)(2,1)S(1)}, bf16[8,128,480]{2,1,0:T(8,128)(2,1)}, u32[]{:S(2)}) copy-start(bf16[8,128,480]{2,1,0:T(8,128)(2,1)} %attend_back.1.gq.a_ref) | copy-start | bytes 2949124
  344.5 28.1 %copy-start.3 = (bf16[8,128,640]{2,1,0:T(8,128)(2,1)S(1)}, bf16[8,128,640]{2,1,0:T(8,128)(2,1)}, u32[]{:S(2)}) copy-start(bf16[8,128,640]{2,1,0:T(8,128)(2,1)} %get-tuple-element.46.a_ref.gp) | copy-start | bytes 3932164
  368.6 5.5 copy-start.4
  370.6 3.5 copy-start.6
  376.2 86.8 %copy-start.10 = (f32[1,2,12,160]{3,1,2,0:T(2,128)S(1)}, f32[1,2,12,160]{3,1,2,0:T(2,128)}, u32[]{:S(2)}) copy-start(f32[1,2,12,160]{3,1,2,0:T(2,128)} %param.19) | copy-start | bytes 46084
  611.2 23.5 %copy-start.11 = (f32[16,256]{1,0:T(8,128)S(1)}, f32[16,256]{1,0:T(8,128)}, u32[]{:S(2)}) copy-start(f32[16,256]{1,0:T(8,128)} %get-tuple-element.65) | copy-start | bytes 49156
  611.2 24.8 %copy-start.8 = (bf16[128,1280]{1,0:T(8,128)(2,1)S(1)}, bf16[128,1280]{1,0:T(8,128)(2,1)}, u32[]{:S(2)}) copy-start(bf16[128,1280]{1,0:T(8,128)(2,1)} %get-tuple-element.146) | copy-start | bytes 983044
  611.2 25.5 %copy-start.7 = (f32[128,1280]{1,0:T(8,128)S(1)}, f32[128,1280]{1,0:T(8,128)}, u32[]{:S(2)}) copy-start(f32[128,1280]{1,0:T(8,128)} %get-tuple-element.147) | copy-start | bytes 1966084
  611.2 26.3 %copy-start.1 = (s32[1,8]{1,0:T(1,128)S(1)}, s32[1,8]{1,0:T(1,128)}, u32[]{:S(2)}) copy-start(s32[1,8]{1,0:T(1,128)} %param.12) | copy-start | bytes 100
